TPU v7x, 32 devices: a whole 2x2x4 slice. The times are simulated.
32 devices in a mesh: dp: 8 (over z, x), tensor: 4 (over y, core).
Axes of the slice: x: 2, y: 2, z: 4, core: 2. Of those that a mesh axis runs over, the one named last changes fastest.
Arguments:
- tokens: bfloat16 [8, 256, 4096], P('dp', 'tensor'), may hold values from -6 to 6
- gain: bfloat16 [4096], replicated, may hold values from 0.5 to 1.5
- wq: bfloat16 [4096, 4096], P(None, 'tensor'), may hold values from -0.09375 to 0.09375
- bq: bfloat16 [4096], P('tensor'), may hold values from -5 to 5
- wkv: bfloat16 [4096, 1024], P(None, 'tensor'), may hold values from -0.09375 to 0.09375
- bkv: bfloat16 [1024], P('tensor'), may hold values from -5 to 5
- wo: bfloat16 [4096, 4096], P('tensor'), may hold values from -0.375 to 0.375
- check_weights: float32 [8, 256], P('dp'), may hold values from -12 to 12
Outputs:
- attended: bfloat16 [8, 256, 4096], P('dp', 'tensor')
- checksum: float32 [4096], replicated
All inputs are finite; a program needn't handle non-finite values.
Results may differ from a plain program's by a relative error of at most 0.018.
Values may be sent and summed in bfloat16 or wider, within the bound.
A program may use at most 64 MiB of HBM per device.

v0:
```python
import jax
import jax.numpy as jnp
from jax import lax
from jax.sharding import PartitionSpec as P

HEADS = 32
KV = 4
HD = 128
EPS = 1e-06
THETA = 1000000.0


def rope(values, head_size):
    rows = values.shape[0]
    half = head_size // 2
    inverse = THETA ** (-(jnp.arange(half, dtype=jnp.float32) * 2.0 / head_size))
    angles = jnp.arange(rows, dtype=jnp.float32)[:, None] * inverse[None, :]
    cosine = jnp.cos(angles)[:, None, :]
    sine = jnp.sin(angles)[:, None, :]
    shaped = values.reshape(rows, -1, head_size)
    first = shaped[..., :half]
    second = shaped[..., half:]
    turned = jnp.concatenate(
        [first * cosine - second * sine, second * cosine + first * sine], axis=-1
    )
    return turned.reshape(rows, -1)


def local(tokens, gain, wq, bq, wkv, bkv, wo, check_weights):
    states = tokens[0].astype(jnp.float32)
    normed = (
        states
        * lax.rsqrt(jnp.mean(states * states, axis=-1, keepdims=True) + EPS)
        * gain.astype(jnp.float32)
    ).astype(jnp.bfloat16)
    position = lax.axis_index("tensor")
    head_dev = wq.shape[1] // HD
    query_cols = head_dev * HD
    shared = position * head_dev // (HEADS // KV)
    joined_w = jnp.concatenate([wq, wkv], axis=1)
    joined_b = jnp.concatenate([bq, bkv], axis=0).astype(jnp.float32)
    projected = (
        jnp.dot(
            lax.all_gather(normed, "tensor", axis=0, tiled=True),
            joined_w,
            preferred_element_type=jnp.float32,
        )
        + joined_b[None, :]
    )
    seq_rows = projected.shape[0]
    query = rope(projected[:, :query_cols], HD).astype(jnp.bfloat16)
    kv_local = projected[:, query_cols:].astype(jnp.bfloat16)
    kv_whole = lax.all_gather(kv_local, "tensor", axis=1, tiled=True)
    key_part = lax.dynamic_slice_in_dim(kv_whole, shared * HD, HD, 1)
    values = lax.dynamic_slice_in_dim(kv_whole, KV * HD + shared * HD, HD, 1)
    keys = rope(key_part.astype(jnp.float32), HD).astype(jnp.bfloat16)
    scale = HD ** (-0.5)
    block = min(512, seq_rows)
    query_heads = query.reshape(seq_rows, head_dev, HD)
    pieces = []
    for number in range(seq_rows // block):
        stop = (number + 1) * block
        query_block = query_heads[number * block : stop]
        scores = (
            jnp.einsum("qhd,kd->hqk", query_block, keys[:stop], preferred_element_type=jnp.float32)
            * scale
        )
        allowed = jnp.arange(block)[:, None] + number * block >= jnp.arange(stop)[None, :]
        scores = jnp.where(allowed[None, :, :], scores, -1e30)
        probs = jax.nn.softmax(scores, axis=-1).astype(jnp.bfloat16)
        mixed = jnp.einsum(
            "hqk,kd->qhd", probs, values[:stop], preferred_element_type=jnp.float32
        ).astype(jnp.bfloat16)
        pieces.append(mixed.reshape(block, query_cols))
    context = jnp.concatenate(pieces, axis=0)
    summed = lax.psum_scatter(
        jnp.dot(context, wo, preferred_element_type=jnp.float32).astype(jnp.bfloat16),
        "tensor",
        scatter_dimension=0,
        tiled=True,
    )
    attended = summed[None, :, :]
    summary = jnp.dot(
        check_weights[0], context.astype(jnp.float32), precision=lax.Precision.HIGHEST
    )
    term = jnp.dot(summary, wo.astype(jnp.float32), precision=lax.Precision.HIGHEST)
    total = lax.psum(term, ("dp", "tensor"))
    checksum = total / jnp.sqrt(jnp.float32(seq_rows * lax.axis_size("dp")))
    return (attended, checksum)


def solution(mesh):
    placed = (
        P("dp", "tensor", None),
        P(),
        P(None, "tensor"),
        P("tensor"),
        P(None, "tensor"),
        P("tensor"),
        P("tensor", None),
        P("dp", None),
    )
    return jax.shard_map(
        local, mesh=mesh, in_specs=placed, out_specs=(P("dp", "tensor", None), P()), check_vma=False
    )
```

profile of v0, /device:TPU:0, one launch (start us, length us, event | category | flops | bytes accessed | tf_op | source)
XLA Modules:
  0.0 118.1 jit_solution(9520385289400516932)
XLA Ops:
  7.2 0.0 copy-start
  7.2 0.0 copy-start.1
  7.2 0.0 copy-start.2
  7.2 0.0 copy-start.3
  7.2 0.0 all-gather.2.cloned.1.call-start
  7.3 0.8 convert_element_type.43
  8.1 1.2 %fusion.9 = f32[64]{0:T(128)S(1)} fusion(bf16[1,64,4096]{2,1,0:T(8,128)(2,1)} %param.8), kind=kLoop, calls=%fused_computation.15 | loop fusion | flops 786368 | bytes 524544 | tf_op jit(solution)/shard_map/reduce_sum | solution.py:33
  9.4 2.0 %fusion.11 = bf16[64,4096]{1,0:T(8,128)(2,1)} fusion(bf16[1,64,4096]{2,1,0:T(8,128)(2,1)} %param.8, f32[4096]{0:T(1024)S(1)} %convert_element_type.43, f32[64]{0:T(128)S(1)} %add_rsqrt_fusion), kind=kLoop, calls=%fused_computation.17 | loop fusion | flops 1048576 | bytes 1065216 | tf_op jit(solution)/shard_map/convert_element_type | solution.py:35
  11.4 0.0 all-gather.2.cloned.1.call-update
  11.4 0.0 reduce-scatter.2.cloned.1.call-start
  11.5 0.0 copy-done.1
  11.5 0.0 copy-done.2
  11.6 0.5 fusion.24
  12.1 24.8 %all-gather.2.cloned.1.call-done = bf16[256,4096]{1,0:T(8,128)(2,1)} async-done(((bf16[64,4096]{1,0:T(8,128)(2,1)}), bf16[256,4096]{1,0:T(8,128)(2,1)}) %all-gather.2.cloned.1.call-update) | async-done | bytes 2097168 | tf_op jit(solution)/shard_map/all_gather | solution.py:44
  36.9 0.0 copy-done.3
  36.9 7.5 %fusion.5 = f32[256,1280]{1,0:T(8,128)S(1)} fusion(bf16[256,4096]{1,0:T(8,128)(2,1)} %all-gather.2.cloned.1.call-done, bf16[4096,256]{1,0:T(8,128)(2,1)S(1)} %copy-done.3, bf16[4096,1024]{1,0:T(8,128)(2,1)} %param.10, f32[1280]{0:T(1024)S(1)} %maximum_convert_fusion), kind=kOutput, calls=%fused_computation.6 | convolution fusion | flops 2705653760 | bytes 13898752 | tf_op jit(solution)/shard_map/dot_general | solution.py:43
  44.4 0.1 slice_bitcast_fusion
  44.5 7.2 %all_gather.7 = bf16[256,1024]{1,0:T(8,128)(2,1)S(1)} all-gather(bf16[256,256]{1,0:T(8,128)(2,1)S(1)} %slice.37), channel_id=1, replica_groups=mesh['dp'=8,'tensor'=4] {'tensor'}, dimensions={1}, use_global_device_ids=true | all-gather | bytes 655360 | tf_op jit(solution)/shard_map/all_gather | solution.py:53
  51.7 0.5 subtract_convert_fusion.1
  52.3 0.2 copy.19
  52.5 0.3 fusion.39
  52.8 0.4 subtract_convert_fusion
  53.2 2.4 %fusion.40 = (f32[8,256]{1,0:T(8,128)S(1)}, f32[8,256,256]{1,2,0:T(8,128)}) fusion(pred[256,256]{0,1:T(8,128)(4,1)S(1)} %iota_compare_fusion, bf16[256,8,64]{2,0,1:T(8,128)(2,1)S(1)} %get-tuple-element.3, bf16[256,8,64]{2,0,1:T(8,128)(2,1)S(1)} %get-tuple-element.2, bf16[256,1,64]{2,0,1:T(8,128)(2,1)S(1)} %get-tuple-element.7, ...), kind=kOutput, calls=%fused_computation.54 | convolution fusion | flops 137494784 | bytes 2760704 | tf_op jit(solution)/shard_map/sub | solution.py:70
  55.6 1.9 %convolution_convert_fusion.1 = bf16[128,8,256]{2,0,1:T(8,128)(2,1)S(1)} fusion(f32[8,256,256]{1,2,0:T(8,128)} %get-tuple-element.11, f32[8,256]{1,0:T(8,128)S(1)} %get-tuple-element.10, bf16[256,1024]{1,0:T(8,128)(2,1)S(1)} %all_gather.7, s32[]{:T(128)S(6)} %select_n.16), kind=kOutput, calls=%fused_computation.13 | convolution fusion | flops 135528448 | bytes 2695172 | tf_op jit(solution)/shard_map/hqk,kd->qhd/dot_general | solution.py:71
  57.5 7.1 %convolution_convert_fusion = bf16[256,4096]{1,0:T(8,128)(2,1)} fusion(bf16[256,1024]{0,1:T(8,128)(2,1)S(1)} %bitcast.49, bf16[1024,4096]{1,0:T(8,128)(2,1)} %param.14), kind=kOutput, calls=%fused_computation.5 | convolution fusion | flops 2148532224 | bytes 11010048 | tf_op jit(solution)/shard_map/dot_general | solution.py:77
  64.6 0.0 reduce-scatter.2.cloned.1.call-update
  64.7 0.0 copy-done
  64.7 0.5 convolution_bitcast_fusion
  65.2 5.7 %fusion.43 = f32[1,4096]{1,0:T(1,128)S(1)} fusion(f32[1024,1]{0,1:T(1,128)S(1)} %convolution_bitcast_fusion, bf16[1024,4096]{1,0:T(8,128)(2,1)} %param.14), kind=kOutput, calls=%fused_computation.55 | convolution fusion | flops 50331648 | bytes 8409088 | tf_op jit(solution)/shard_map/dot_general | solution.py:86
  70.9 39.7 %psum.7 = f32[4096]{0:T(1024)S(1)} all-reduce(f32[4096]{0:T(1024)S(1)} %bitcast.51), channel_id=1, replica_groups=mesh['dp'=8,'tensor'=4] {'dp','tensor'}, use_global_device_ids=true, to_apply=%region_4.5 | all-reduce | flops 4096 | bytes 32768 | tf_op jit(solution)/shard_map/psum | solution.py:87
  110.6 0.6 broadcast_multiply_fusion
  111.2 0.0 reduce-scatter.2.cloned.1.call-done
  (6 shorter events, 0.1 us)
Async XLA Ops:
  7.2 57.5 %copy-start = (f32[1,256]{1,0:T(1,128)S(1)}, f32[1,256]{1,0:T(1,128)}, u32[]{:S(2)}) copy-start(f32[1,256]{1,0:T(1,128)} %param.15) | copy-start | bytes 3076
  7.2 4.3 %copy-start.1 = (bf16[1024]{0:T(1024)(128)(2,1)S(1)}, bf16[1024]{0:T(1024)(128)(2,1)}, u32[]{:S(2)}) copy-start(bf16[1024]{0:T(1024)(128)(2,1)} %param.11) | copy-start | bytes 6148
  7.2 4.3 %copy-start.2 = (bf16[256]{0:T(256)(128)(2,1)S(1)}, bf16[256]{0:T(256)(128)(2,1)}, u32[]{:S(2)}) copy-start(bf16[256]{0:T(256)(128)(2,1)} %param.13) | copy-start | bytes 1540
  7.2 29.7 %copy-start.3 = (bf16[4096,256]{1,0:T(8,128)(2,1)S(1)}, bf16[4096,256]{1,0:T(8,128)(2,1)}, u32[]{:S(2)}) copy-start(bf16[4096,256]{1,0:T(8,128)(2,1)} %param.12) | copy-start | bytes 6291460
  7.2 29.7 %all-gather.2.cloned.1.call-start = ((), (), s32[]{:S(2)}) async-start(), calls=%async_computation.1 | async-start | bytes 2621440 | tf_op jit(solution)/shard_map/all_gather | solution.py:44
  11.4 99.8 %reduce-scatter.2.cloned.1.call-start = ((), (), s32[]{:S(2)}) async-start(), calls=%async_computation.2 | async-start | bytes 2621440 | tf_op jit(solution)/shard_map/reduce_scatter | solution.py:76
Sparse Core Ops, SparseCore 0:
  11.5 25.2 all-gather.1
  64.8 31.3 reduce-scatter.1
where the time goes:
time: 118 us
  blocking collectives  46.9 us (40%)
  matrix products  25.1 us (21%)
  waiting for transfers between devices  24.8 us (21%)
  between operations  14.2 us (12%)
  other arithmetic  6.25 us (5%)
    psum x1, blocking collectives, local(): total = lax.psum(term, ('dp', 'tensor'))  39.7 us
    all_gather x1, waiting for transfers between devices, local(): lax.all_gather(normed, 'tensor', axis=0, tiled=True)  24.8 us
    dot_general x1, matrix products, local(): jnp.dot(lax.all_gather(normed, 'tensor', axis=0, tiled=True), joined_w, p...  7.53 us
    all_gather x1, blocking collectives, local(): kv_whole = lax.all_gather(kv_local, 'tensor', axis=1, tiled=True)  7.16 us
    dot_general x1, matrix products, local(): jnp.dot(context, wo, preferred_element_type=jnp.float32)  7.11 us
    dot_general x1, matrix products, local(): jnp.dot(summary, wo.astype(jnp.float32), precision=lax.Precision.HIGHEST)  5.68 us
  transfers between devices with their start and end apart: 2, of which 1 were waited for; matrix products, arithmetic and copies ran while one was open for 6% of the time, Pallas kernels for 0%

commit v1 on v0

--- a/solution.py
+++ b/solution.py
@@ -84,7 +84,7 @@
         check_weights[0], context.astype(jnp.float32), precision=lax.Precision.HIGHEST
     )
     term = jnp.dot(summary, wo.astype(jnp.float32), precision=lax.Precision.HIGHEST)
-    total = lax.psum(term, ("dp", "tensor"))
+    total = lax.psum(lax.psum(term, "tensor"), "dp")
     checksum = total / jnp.sqrt(jnp.float32(seq_rows * lax.axis_size("dp")))
     return (attended, checksum)
 

time: 118 us -> 126 us (1.068)
  blocking collectives: 46.9 us -> 54.7 us
    psum x1 -> x2, blocking collectives: 39.7 us -> 47.5 us  [local(): total = lax.psum(lax.psum(term, 'tensor'), 'dp')]
where the time goes in v1:
time: 126 us
  blocking collectives  54.7 us (43%)
  matrix products  25.1 us (20%)
  waiting for transfers between devices  24.8 us (20%)
  between operations  14.2 us (11%)
  other arithmetic  6.25 us (5%)
    psum x2, blocking collectives, local(): total = lax.psum(lax.psum(term, 'tensor'), 'dp')  47.5 us
    all_gather x1, waiting for transfers between devices, local(): lax.all_gather(normed, 'tensor', axis=0, tiled=True)  24.8 us
    dot_general x1, matrix products, local(): jnp.dot(lax.all_gather(normed, 'tensor', axis=0, tiled=True), joined_w, p...  7.53 us
    all_gather x1, blocking collectives, local(): kv_whole = lax.all_gather(kv_local, 'tensor', axis=1, tiled=True)  7.16 us
    dot_general x1, matrix products, local(): jnp.dot(context, wo, preferred_element_type=jnp.float32)  7.12 us
    dot_general x1, matrix products, local(): jnp.dot(summary, wo.astype(jnp.float32), precision=lax.Precision.HIGHEST)  5.68 us
  transfers between devices with their start and end apart: 2, of which 1 were waited for; matrix products, arithmetic and copies ran while one was open for 6% of the time, Pallas kernels for 0%

profile of v1, /device:TPU:0, one launch (start us, length us, event | category | flops | bytes accessed | tf_op | source)
XLA Modules:
  0.0 125.9 jit_solution(10651515179446965862)
XLA Ops:
  7.2 0.0 copy-start
  7.2 0.0 copy-start.1
  7.2 0.0 copy-start.2
  7.2 0.0 copy-start.3
  7.2 0.0 all-gather.2.cloned.1.call-start
  7.3 0.8 convert_element_type.43
  8.1 1.2 fusion.9
  9.4 2.0 %fusion.11 = bf16[64,4096]{1,0:T(8,128)(2,1)} fusion(bf16[1,64,4096]{2,1,0:T(8,128)(2,1)} %param.8, f32[4096]{0:T(1024)S(1)} %convert_element_type.43, f32[64]{0:T(128)S(1)} %add_rsqrt_fusion), kind=kLoop, calls=%fused_computation.17 | loop fusion | flops 1048576 | bytes 1065216 | tf_op jit(solution)/shard_map/convert_element_type | solution.py:35
  11.4 0.0 all-gather.2.cloned.1.call-update
  11.4 0.0 reduce-scatter.2.cloned.1.call-start
  11.5 0.0 copy-done.1
  11.5 0.0 copy-done.2
  11.6 0.5 fusion.24
  12.1 24.8 %all-gather.2.cloned.1.call-done = bf16[256,4096]{1,0:T(8,128)(2,1)} async-done(((bf16[64,4096]{1,0:T(8,128)(2,1)}), bf16[256,4096]{1,0:T(8,128)(2,1)}) %all-gather.2.cloned.1.call-update) | async-done | bytes 2097168 | tf_op jit(solution)/shard_map/all_gather | solution.py:44
  36.9 0.0 copy-done.3
  36.9 7.5 %fusion.5 = f32[256,1280]{1,0:T(8,128)S(1)} fusion(bf16[256,4096]{1,0:T(8,128)(2,1)} %all-gather.2.cloned.1.call-done, bf16[4096,256]{1,0:T(8,128)(2,1)S(1)} %copy-done.3, bf16[4096,1024]{1,0:T(8,128)(2,1)} %param.10, f32[1280]{0:T(1024)S(1)} %maximum_convert_fusion), kind=kOutput, calls=%fused_computation.6 | convolution fusion | flops 2705653760 | bytes 13898752 | tf_op jit(solution)/shard_map/dot_general | solution.py:43
  44.4 0.1 slice_bitcast_fusion
  44.5 7.2 %all_gather.7 = bf16[256,1024]{1,0:T(8,128)(2,1)S(1)} all-gather(bf16[256,256]{1,0:T(8,128)(2,1)S(1)} %slice.37), channel_id=1, replica_groups=mesh['dp'=8,'tensor'=4] {'tensor'}, dimensions={1}, use_global_device_ids=true | all-gather | bytes 655360 | tf_op jit(solution)/shard_map/all_gather | solution.py:53
  51.7 0.5 subtract_convert_fusion.1
  52.3 0.2 copy.19
  52.5 0.3 fusion.39
  52.8 0.4 subtract_convert_fusion
  53.2 2.4 %fusion.40 = (f32[8,256]{1,0:T(8,128)S(1)}, f32[8,256,256]{1,2,0:T(8,128)}) fusion(pred[256,256]{0,1:T(8,128)(4,1)S(1)} %iota_compare_fusion, bf16[256,8,64]{2,0,1:T(8,128)(2,1)S(1)} %get-tuple-element.3, bf16[256,8,64]{2,0,1:T(8,128)(2,1)S(1)} %get-tuple-element.2, bf16[256,1,64]{2,0,1:T(8,128)(2,1)S(1)} %get-tuple-element.7, ...), kind=kOutput, calls=%fused_computation.54 | convolution fusion | flops 137494784 | bytes 2760704 | tf_op jit(solution)/shard_map/sub | solution.py:70
  55.6 1.9 %convolution_convert_fusion.1 = bf16[128,8,256]{2,0,1:T(8,128)(2,1)S(1)} fusion(f32[8,256,256]{1,2,0:T(8,128)} %get-tuple-element.11, f32[8,256]{1,0:T(8,128)S(1)} %get-tuple-element.10, bf16[256,1024]{1,0:T(8,128)(2,1)S(1)} %all_gather.7, s32[]{:T(128)S(6)} %select_n.16), kind=kOutput, calls=%fused_computation.13 | convolution fusion | flops 135528448 | bytes 2695172 | tf_op jit(solution)/shard_map/hqk,kd->qhd/dot_general | solution.py:71
  57.5 7.1 %convolution_convert_fusion = bf16[256,4096]{1,0:T(8,128)(2,1)} fusion(bf16[256,1024]{0,1:T(8,128)(2,1)S(1)} %bitcast.49, bf16[1024,4096]{1,0:T(8,128)(2,1)} %param.14), kind=kOutput, calls=%fused_computation.5 | convolution fusion | flops 2148532224 | bytes 11010048 | tf_op jit(solution)/shard_map/dot_general | solution.py:77
  64.6 0.0 reduce-scatter.2.cloned.1.call-update
  64.7 0.0 copy-done
  64.7 0.5 convolution_bitcast_fusion
  65.2 5.7 %fusion.43 = f32[1,4096]{1,0:T(1,128)S(1)} fusion(f32[1024,1]{0,1:T(1,128)S(1)} %convolution_bitcast_fusion, bf16[1024,4096]{1,0:T(8,128)(2,1)} %param.14), kind=kOutput, calls=%fused_computation.55 | convolution fusion | flops 50331648 | bytes 8409088 | tf_op jit(solution)/shard_map/dot_general | solution.py:86
  70.9 10.5 %psum.14 = f32[4096]{0:T(1024)S(1)} all-reduce(f32[4096]{0:T(1024)S(1)} %bitcast.51), channel_id=1, replica_groups=mesh['dp'=8,'tensor'=4] {'tensor'}, use_global_device_ids=true, to_apply=%region_4.5 | all-reduce | flops 4096 | bytes 32768 | tf_op jit(solution)/shard_map/psum | solution.py:87
  81.3 37.1 %psum.15 = f32[4096]{0:T(1024)S(1)} all-reduce(f32[4096]{0:T(1024)S(1)} %psum.14), channel_id=1, replica_groups=mesh['dp'=8,'tensor'=4] {'dp'}, use_global_device_ids=true, to_apply=%region_5.6 | all-reduce | flops 4096 | bytes 32768 | tf_op jit(solution)/shard_map/psum | solution.py:87
  118.4 0.6 broadcast_multiply_fusion
  (7 shorter events, 0.1 us)
Async XLA Ops:
  7.2 57.5 %copy-start = (f32[1,256]{1,0:T(1,128)S(1)}, f32[1,256]{1,0:T(1,128)}, u32[]{:S(2)}) copy-start(f32[1,256]{1,0:T(1,128)} %param.15) | copy-start | bytes 3076
  7.2 4.3 %copy-start.1 = (bf16[1024]{0:T(1024)(128)(2,1)S(1)}, bf16[1024]{0:T(1024)(128)(2,1)}, u32[]{:S(2)}) copy-start(bf16[1024]{0:T(1024)(128)(2,1)} %param.11) | copy-start | bytes 6148
  7.2 4.3 %copy-start.2 = (bf16[256]{0:T(256)(128)(2,1)S(1)}, bf16[256]{0:T(256)(128)(2,1)}, u32[]{:S(2)}) copy-start(bf16[256]{0:T(256)(128)(2,1)} %param.13) | copy-start | bytes 1540
  7.2 29.7 %copy-start.3 = (bf16[4096,256]{1,0:T(8,128)(2,1)S(1)}, bf16[4096,256]{1,0:T(8,128)(2,1)}, u32[]{:S(2)}) copy-start(bf16[4096,256]{1,0:T(8,128)(2,1)} %param.12) | copy-start | bytes 6291460
  7.2 29.7 %all-gather.2.cloned.1.call-start = ((), (), s32[]{:S(2)}) async-start(), calls=%async_computation.1 | async-start | bytes 2621440 | tf_op jit(solution)/shard_map/all_gather | solution.py:44
  11.4 107.6 %reduce-scatter.2.cloned.1.call-start = ((), (), s32[]{:S(2)}) async-start(), calls=%async_computation.2 | async-start | bytes 2621440 | tf_op jit(solution)/shard_map/reduce_scatter | solution.py:76
Sparse Core Ops, SparseCore 0:
  11.5 25.2 all-gather.1
  64.8 31.1 reduce-scatter.1
